TPU v7x, 32 devices: a whole 2x2x4 slice. The times are simulated.
32 devices in a mesh: rows: 8 (over z, y), mem: 4 (over x, core).
Axes of the slice: x: 2, y: 2, z: 4, core: 2. Of those that a mesh axis runs over, the one named last changes fastest.
Arguments:
- ensemble: float32 [64, 32, 48, 384], P('mem', None, 'rows'), may hold values from 0 to 2
- courant: float32 [3, 32, 48, 384], P(None, None, 'rows'), may hold values from -0.22 to 0.22
- obs_column: int32 [128], P('rows'), may hold values from 0 to 18431, as said below
- obs_value: float32 [32, 128], P(None, 'rows'), may hold values from -6 to 6
- obs_var: float32 [32, 128], P(None, 'rows'), may hold values from 0.5 to 8
Outputs:
- analysis: float32 [64, 32, 48, 384], P('mem', None, 'rows')
Inputs may be any that keep to these rules, and one draw needn't show every extreme that they name: `obs_column`: entry p is x * 384 + y with x from (p // 16) * 6 to (p // 16) * 6 + 5.
All inputs are finite; a program needn't handle non-finite values.
Results may differ from a plain program's by a relative error of at most 0.0003.
Values sent between devices are 32-bit elements; how exact they have to be, the bound alone decides.
A program may use at most 128 MiB of HBM per device.

v0:
```python
import jax
import jax.numpy as jnp
from jax import lax
from jax.sharding import PartitionSpec as P

STEPS = 3
NS_ITERS = 4


DIFFUSION = 0.05


def padded_2(cells, sides, width):
    for axis, dim in sides:
        count = lax.axis_size(axis)
        ends = count - 1
        head = lax.slice_in_dim(cells, 0, width, axis=dim)
        tail = lax.slice_in_dim(cells, cells.shape[dim] - width, cells.shape[dim], axis=dim)
        cells = jnp.concatenate(
            [
                lax.ppermute(tail, axis, [(i, (i + 1) % count) for i in range(ends)]),
                cells,
                lax.ppermute(head, axis, [((i + 1) % count, i) for i in range(ends)]),
            ],
            axis=dim,
        )
    return cells


def advance(padded, courant):
    center = padded[:, :, 1:-1, :]
    below_x = padded[:, :, :-2, :]
    above_x = padded[:, :, 2:, :]
    padded_y = jnp.pad(center, ((0, 0), (0, 0), (0, 0), (1, 1)))
    below_y = padded_y[:, :, :, :-2]
    above_y = padded_y[:, :, :, 2:]
    padded_z = jnp.pad(center, ((0, 0), (1, 1), (0, 0), (0, 0)))
    below_z = padded_z[:, :-2]
    above_z = padded_z[:, 2:]
    change = jnp.zeros_like(center)
    for component, below, above in (
        (0, below_x, above_x),
        (1, below_y, above_y),
        (2, below_z, above_z),
    ):
        velocity = courant[component][None]
        change = (
            change
            - jnp.maximum(velocity, 0.0) * (center - below)
            - jnp.minimum(velocity, 0.0) * (above - center)
            + DIFFUSION * (above + below - 2.0 * center)
        )
    return center + change


def gram_terms(profiles, obs_value, obs_var):
    members_all = profiles.shape[0]
    center = jnp.mean(profiles, axis=0)
    scaling = 1.0 / jnp.sqrt((members_all - 1.0) * obs_var)
    scaled = ((profiles - center[None]) * scaling[None]).reshape(members_all, -1)
    innovation = ((obs_value - center) / jnp.sqrt(obs_var)).reshape(-1)
    gram_part = jnp.dot(scaled, scaled.T, precision=lax.Precision.HIGHEST)
    pull_part = jnp.dot(scaled, innovation, precision=lax.Precision.HIGHEST)
    return (gram_part, pull_part)


def mixing(gram_sum, pull_sum):
    members_all = gram_sum.shape[0]
    identity_matrix = jnp.eye(members_all, dtype=jnp.float32)
    system = identity_matrix + gram_sum
    frobenius = jnp.sqrt(jnp.sum(system * system))

    def newton(iteration, carry):
        iterate, inverse_root = carry
        factor = 0.5 * (
            3.0 * identity_matrix - jnp.dot(inverse_root, iterate, precision=lax.Precision.HIGHEST)
        )
        return (
            jnp.dot(iterate, factor, precision=lax.Precision.HIGHEST),
            jnp.dot(factor, inverse_root, precision=lax.Precision.HIGHEST),
        )

    iterate, inverse_root = lax.fori_loop(
        0, NS_ITERS, newton, (system / frobenius, identity_matrix)
    )
    root_inverse = inverse_root / jnp.sqrt(frobenius)
    mean_shift = jnp.dot(
        root_inverse,
        jnp.dot(root_inverse, pull_sum, precision=lax.Precision.HIGHEST),
        precision=lax.Precision.HIGHEST,
    ) / jnp.sqrt(members_all - 1.0)
    centering = identity_matrix - 1.0 / members_all
    return 1.0 / members_all + jnp.dot(
        centering, mean_shift[:, None] + root_inverse, precision=lax.Precision.HIGHEST
    )


def per_device(ensemble, courant, obs_column, obs_value, obs_var):
    rows_local = ensemble.shape[2]
    width_y = ensemble.shape[3]
    position = lax.axis_index("rows")
    concentration = ensemble
    for step_index in range(STEPS):
        padded = padded_2(concentration, (("rows", 2),), 1)
        concentration = advance(padded, courant)
    members_dev = concentration.shape[0]
    state_vectors = concentration.reshape(members_dev, concentration.shape[1], rows_local * width_y)
    local_column = obs_column - position * (rows_local * width_y)
    profiles = jnp.take(state_vectors, local_column, axis=2)
    gathered = lax.all_gather(profiles, "mem", axis=0, tiled=True)
    gram_part, pull_part = gram_terms(gathered, obs_value, obs_var)
    gram_sum, pull_sum = lax.psum((gram_part, pull_part), "rows")
    transform_weights = mixing(gram_sum, pull_sum)
    first_member = lax.axis_index("mem") * members_dev
    own_columns = lax.dynamic_slice_in_dim(transform_weights, first_member, members_dev, 1)
    updated_ensemble = jnp.einsum(
        "jk,jzc->kzc",
        own_columns,
        lax.all_gather(state_vectors, "mem", axis=0, tiled=True),
        precision=lax.Precision.HIGHEST,
    )
    return updated_ensemble.reshape(concentration.shape)


def solution(mesh):
    return jax.shard_map(
        per_device,
        mesh=mesh,
        in_specs=(
            P("mem", None, "rows", None),
            P(None, None, "rows", None),
            P("rows"),
            P(None, "rows"),
            P(None, "rows"),
        ),
        out_specs=P("mem", None, "rows", None),
        check_vma=False,
    )
```

profile of v0, /device:TPU:0, one launch (start us, length us, event | category | flops | bytes accessed | tf_op | source)
XLA Modules:
  0.0 316.3 jit_solution(4887929447039893522)
XLA Ops:
  6.5 1.6 fusion.82
  8.2 5.1 %collective-permute-start = (f32[16,32,1,384]{3,1,2,0:T(8,128)S(1)}, f32[16,32,1,384]{3,1,2,0:T(8,128)S(1)}, u32[]{:S(2)}, u32[]{:S(2)}) collective-permute-start(f32[16,32,1,384]{3,1,2,0:T(8,128)S(1)} %get-tuple-element.56), channel_id=1, source_target_pairs={{0,4},{4,8},{8,12},{12,16},{16,20},{20,24},{24,28},{1,5},{5,9},{9,... | collective-permute-start | bytes 2359304 | tf_op jit(solution)/shard_map/ppermute | solution.py:21
  13.3 1.3 collective-permute-start.1
  14.6 1.3 maximum_bitcast_fusion.2
  15.9 30.9 %collective-permute-done = f32[16,32,1,384]{3,1,2,0:T(8,128)S(1)} collective-permute-done((f32[16,32,1,384]{3,1,2,0:T(8,128)S(1)}, f32[16,32,1,384]{3,1,2,0:T(8,128)S(1)}, u32[]{:S(2)}, u32[]{:S(2)}) %collective-permute-start) | collective-permute-done | bytes 786464 | tf_op jit(solution)/shard_map/ppermute | solution.py:21
  46.9 8.0 %fusion.49 = f32[16,32,6,384]{3,1,2,0:T(8,128)S(1)} fusion(f32[16,32,6,384]{3,1,2,0:T(8,128)S(1)} %copy-done.1, f32[16,32,1,384]{3,1,2,0:T(8,128)S(1)} %collective-permute-done.1, f32[16,32,1,384]{3,1,2,0:T(8,128)S(1)} %collective-permute-done, f32[32,6,384]{2,0,1:T(8,128)S(1)} %get-tuple-element.61, f32[32,6,384]{2,0,1:T(8,128)S(1)} %get-tuple-element.62, ...), kind=kLoop, calls=%fused_computation.69 | loop fusion | flops 40108032 | bytes 12779520 | tf_op jit(solution)/shard_map/add | solution.py:53
  54.9 0.1 fusion.81
  55.0 4.4 %collective-permute-start.2 = (f32[16,32,1,384]{3,1,2,0:T(8,128)S(1)}, f32[16,32,1,384]{3,1,2,0:T(8,128)S(1)}, u32[]{:S(2)}, u32[]{:S(2)}) collective-permute-start(f32[16,32,1,384]{3,1,2,0:T(8,128)S(1)} %get-tuple-element.54), channel_id=1, source_target_pairs={{0,4},{4,8},{8,12},{12,16},{16,20},{20,24},{24,28},{1,5},{5,9},{9,... | collective-permute-start | bytes 2359304 | tf_op jit(solution)/shard_map/ppermute | solution.py:21
  59.4 1.3 collective-permute-start.3
  60.7 31.4 %collective-permute-done.2 = f32[16,32,1,384]{3,1,2,0:T(8,128)S(1)} collective-permute-done((f32[16,32,1,384]{3,1,2,0:T(8,128)S(1)}, f32[16,32,1,384]{3,1,2,0:T(8,128)S(1)}, u32[]{:S(2)}, u32[]{:S(2)}) %collective-permute-start.2) | collective-permute-done | bytes 786464 | tf_op jit(solution)/shard_map/ppermute | solution.py:21
  92.1 8.0 %fusion.32 = f32[16,32,6,384]{3,1,2,0:T(8,128)S(1)} fusion(f32[16,32,6,384]{3,1,2,0:T(8,128)S(1)} %fusion.49, f32[16,32,1,384]{3,1,2,0:T(8,128)S(1)} %collective-permute-done.3, f32[16,32,1,384]{3,1,2,0:T(8,128)S(1)} %collective-permute-done.2, f32[32,6,384]{2,0,1:T(8,128)S(1)} %get-tuple-element.61, f32[32,6,384]{2,0,1:T(8,128)S(1)} %get-tuple-element.62, ...), kind=kLoop, calls=%fused_computation.50 | loop fusion | flops 40108032 | bytes 12779520 | tf_op jit(solution)/shard_map/add | solution.py:53
  100.1 0.1 fusion.80
  100.3 4.4 %collective-permute-start.4 = (f32[16,32,1,384]{3,1,2,0:T(8,128)S(1)}, f32[16,32,1,384]{3,1,2,0:T(8,128)S(1)}, u32[]{:S(2)}, u32[]{:S(2)}) collective-permute-start(f32[16,32,1,384]{3,1,2,0:T(8,128)S(1)} %get-tuple-element.52), channel_id=1, source_target_pairs={{0,4},{4,8},{8,12},{12,16},{16,20},{20,24},{24,28},{1,5},{5,9},{9,... | collective-permute-start | bytes 2359304 | tf_op jit(solution)/shard_map/ppermute | solution.py:21
  104.7 1.3 collective-permute-start.5
  106.0 30.6 %collective-permute-done.4 = f32[16,32,1,384]{3,1,2,0:T(8,128)S(1)} collective-permute-done((f32[16,32,1,384]{3,1,2,0:T(8,128)S(1)}, f32[16,32,1,384]{3,1,2,0:T(8,128)S(1)}, u32[]{:S(2)}, u32[]{:S(2)}) %collective-permute-start.4) | collective-permute-done | bytes 786464 | tf_op jit(solution)/shard_map/ppermute | solution.py:21
  136.6 8.0 %fusion.15 = f32[16,6,4,8,384]{4,3,2,1,0:T(8,128)S(1)} fusion(f32[16,32,6,384]{3,1,2,0:T(8,128)S(1)} %fusion.32, f32[16,32,1,384]{3,1,2,0:T(8,128)S(1)} %collective-permute-done.5, f32[16,32,1,384]{3,1,2,0:T(8,128)S(1)} %collective-permute-done.4, f32[32,6,384]{2,0,1:T(8,128)S(1)} %get-tuple-element.61, f32[32,6,384]{2,0,1:T(8,128)S(1)} %get-tuple-element.62, ...), kind=kLoop, calls=%fused_computation.31 | loop fusion | flops 40108032 | bytes 12779520
  144.6 0.4 copy.26
  145.0 2.1 copy-done
  147.1 4.9 %copy.18 = f32[16,32,2304]{2,0,1:T(8,128)} copy(f32[16,32,2304]{2,1,0:T(8,128)S(1)} %bitcast.64) | data formatting | bytes 9437184 | tf_op jit(solution)/shard_map/reshape | solution.py:107
  152.1 0.6 copy-done.4
  152.8 14.0 %copy.14 = f32[16,32,2304]{1,0,2:T(8,128)} copy(f32[16,32,2304]{2,1,0:T(8,128)} %bitcast.65) | data formatting | bytes 9437184 | tf_op jit(solution)/shard_map/reshape | solution.py:107
  166.7 10.4 %gather_fusion = f32[16,16,32]{2,1,0:T(8,128)S(1)} fusion(f32[16,32,2304]{1,0,2:T(8,128)} %copy.14, s32[1024]{0:T(1024)S(1)} %pad_clamp_fusion), kind=kCustom, calls=%fused_computation | custom fusion | bytes 65600 | tf_op jit(solution)/shard_map/jit(_take)/gather | solution.py:109
  177.2 0.1 select_bitcast_fusion
  177.2 10.5 %all_gather.6 = f32[64,32,16]{1,0,2:T(8,128)S(1)} all-gather(f32[16,32,16]{1,0,2:T(8,128)S(1)} %select_bitcast_fusion), channel_id=1, replica_groups=mesh['rows'=8,'mem'=4] {'mem'}, dimensions={0}, use_global_device_ids=true | all-gather | bytes 163840 | tf_op jit(solution)/shard_map/all_gather | solution.py:110
  187.8 0.5 convolution_bitcast_fusion.4
  188.4 0.6 convolution_bitcast_fusion.1
  189.0 42.6 %all-reduce.6 = (f32[64]{0:T(128)S(1)}, f32[64,64]{1,0:T(8,128)S(1)}) all-reduce(f32[64]{0:T(128)S(1)} %convolution_bitcast_fusion.4, f32[64,64]{1,0:T(8,128)S(1)} %convolution_bitcast_fusion.1), channel_id=1, replica_groups=mesh['rows'=8,'mem'=4] {'rows'}, use_global_device_ids=true, to_apply=%region_5.6 | all-reduce | flops 4160 | bytes 33280 | tf_op jit(solution)/shard_map/psum | solution.py:112
  231.6 0.7 multiply_reduce_fusion
  233.0 2.6 while.13
  233.0 0.2 fusion.107
  233.2 0.2 fusion.108
  233.4 0.2 convolution_bitcast_fusion.6
  233.7 0.2 fusion.107
  233.9 0.2 fusion.108
  234.1 0.2 convolution_bitcast_fusion.6
  234.3 0.2 fusion.107
  234.5 0.2 fusion.108
  234.7 0.2 convolution_bitcast_fusion.6
  235.0 0.2 fusion.107
  235.2 0.2 fusion.108
  235.3 0.2 convolution_bitcast_fusion.6
  235.6 0.2 convolution_bitcast_fusion.3
  235.8 0.2 fusion.58
  235.9 0.3 fusion.63
  236.3 45.6 %all-gather.2.cloned.1.call-done = f32[64,32,2304]{2,0,1:T(8,128)} async-done(((f32[16,32,2304]{2,0,1:T(8,128)}), f32[64,32,2304]{2,0,1:T(8,128)}) %all-gather.2.cloned.1.call-update) | async-done | bytes 18874384 | tf_op jit(solution)/shard_map/all_gather | solution.py:119
  281.8 13.4 %fusion.73 = f32[16,32,2304]{2,0,1:T(8,128)} fusion(f32[64,32,2304]{2,0,1:T(8,128)} %all-gather.2.cloned.1.call-done, f32[64,64]{0,1:T(8,128)S(1)} %fusion.63, s32[]{:T(128)S(6)} %select_n.14), kind=kOutput, calls=%fused_computation.112 | convolution fusion | flops 905970688 | bytes 23601156 | tf_op jit(solution)/shard_map/jk,jzc->kzc/dot_general | solution.py:116
  295.2 6.5 %reshape.37 = f32[16,32,6,384]{3,2,0,1:T(8,128)} reshape(f32[16,32,2304]{2,0,1:T(8,128)} %fusion.73) | data formatting | bytes 9437184 | tf_op jit(solution)/shard_map/reshape | solution.py:122
  301.8 7.7 %copy.20 = f32[16,32,6,384]{3,1,2,0:T(8,128)} copy(f32[16,32,6,384]{3,2,0,1:T(8,128)} %reshape.37) | data formatting | bytes 9437184 | tf_op jit(solution)/shard_map/reshape | solution.py:122
  (28 shorter events, 0.2 us)
Async XLA Ops:
  6.5 275.3 %all-gather.2.cloned.1.call-start = ((), (), s32[]{:S(2)}) async-start(), calls=%async_computation | async-start | bytes 23592960 | tf_op jit(solution)/shard_map/all_gather | solution.py:119
  6.5 40.3 %copy-start.1 = (f32[16,32,6,384]{3,1,2,0:T(8,128)S(1)}, f32[16,32,6,384]{3,1,2,0:T(8,128)}, u32[]{:S(2)}) copy-start(f32[16,32,6,384]{3,1,2,0:T(8,128)} %param.7) | copy-start | bytes 14155780
  8.2 38.7 %collective-permute-start = (f32[16,32,1,384]{3,1,2,0:T(8,128)S(1)}, f32[16,32,1,384]{3,1,2,0:T(8,128)S(1)}, u32[]{:S(2)}, u32[]{:S(2)}) collective-permute-start(f32[16,32,1,384]{3,1,2,0:T(8,128)S(1)} %get-tuple-element.56), channel_id=1, source_target_pairs={{0,4},{4,8},{8,12},{12,16},{16,20},{20,24},{24,28},{1,5},{5,9},{9,... | collective-permute-start | bytes 2359304 | tf_op jit(solution)/shard_map/ppermute | solution.py:21
  13.3 33.6 %collective-permute-start.1 = (f32[16,32,1,384]{3,1,2,0:T(8,128)S(1)}, f32[16,32,1,384]{3,1,2,0:T(8,128)S(1)}, u32[]{:S(2)}, u32[]{:S(2)}) collective-permute-start(f32[16,32,1,384]{3,1,2,0:T(8,128)S(1)} %get-tuple-element.57), channel_id=1, source_target_pairs={{4,0},{8,4},{12,8},{16,12},{20,16},{24,20},{28,24},{5,1},{9,5},{13... | collective-permute-start | bytes 2359304 | tf_op jit(solution)/shard_map/ppermute | solution.py:23
  55.0 37.2 %collective-permute-start.2 = (f32[16,32,1,384]{3,1,2,0:T(8,128)S(1)}, f32[16,32,1,384]{3,1,2,0:T(8,128)S(1)}, u32[]{:S(2)}, u32[]{:S(2)}) collective-permute-start(f32[16,32,1,384]{3,1,2,0:T(8,128)S(1)} %get-tuple-element.54), channel_id=1, source_target_pairs={{0,4},{4,8},{8,12},{12,16},{16,20},{20,24},{24,28},{1,5},{5,9},{9,... | collective-permute-start | bytes 2359304 | tf_op jit(solution)/shard_map/ppermute | solution.py:21
  59.4 32.7 %collective-permute-start.3 = (f32[16,32,1,384]{3,1,2,0:T(8,128)S(1)}, f32[16,32,1,384]{3,1,2,0:T(8,128)S(1)}, u32[]{:S(2)}, u32[]{:S(2)}) collective-permute-start(f32[16,32,1,384]{3,1,2,0:T(8,128)S(1)} %get-tuple-element.55), channel_id=1, source_target_pairs={{4,0},{8,4},{12,8},{16,12},{20,16},{24,20},{28,24},{5,1},{9,5},{13... | collective-permute-start | bytes 2359304 | tf_op jit(solution)/shard_map/ppermute | solution.py:23
  100.3 36.3 %collective-permute-start.4 = (f32[16,32,1,384]{3,1,2,0:T(8,128)S(1)}, f32[16,32,1,384]{3,1,2,0:T(8,128)S(1)}, u32[]{:S(2)}, u32[]{:S(2)}) collective-permute-start(f32[16,32,1,384]{3,1,2,0:T(8,128)S(1)} %get-tuple-element.52), channel_id=1, source_target_pairs={{0,4},{4,8},{8,12},{12,16},{16,20},{20,24},{24,28},{1,5},{5,9},{9,... | collective-permute-start | bytes 2359304 | tf_op jit(solution)/shard_map/ppermute | solution.py:21
  104.7 31.9 %collective-permute-start.5 = (f32[16,32,1,384]{3,1,2,0:T(8,128)S(1)}, f32[16,32,1,384]{3,1,2,0:T(8,128)S(1)}, u32[]{:S(2)}, u32[]{:S(2)}) collective-permute-start(f32[16,32,1,384]{3,1,2,0:T(8,128)S(1)} %get-tuple-element.53), channel_id=1, source_target_pairs={{4,0},{8,4},{12,8},{16,12},{20,16},{24,20},{28,24},{5,1},{9,5},{13... | collective-permute-start | bytes 2359304 | tf_op jit(solution)/shard_map/ppermute | solution.py:23
  145.0 2.2 copy-start
  152.1 0.7 copy-start.4
  152.8 35.0 %copy-start.2 = (f32[32,16]{0,1:T(8,128)S(1)}, f32[32,16]{0,1:T(8,128)}, u32[]{:S(2)}) copy-start(f32[32,16]{0,1:T(8,128)} %param.11) | copy-start | bytes 6148
  152.8 35.0 %copy-start.3 = (f32[32,16]{0,1:T(8,128)S(1)}, f32[32,16]{0,1:T(8,128)}, u32[]{:S(2)}) copy-start(f32[32,16]{0,1:T(8,128)} %param.10) | copy-start | bytes 6148
Sparse Core Ops, SparseCore 0:
  152.2 129.5 all-gather.1
where the time goes:
time: 317 us; the launch traced here: 316 us
  waiting for transfers between devices  139 us (44%)
  blocking collectives  53.1 us (17%)
  local copies, waits for them, and re-layouts  48.7 us (15%)
  other arithmetic  26.2 us (8%)
  starting transfers between devices  17.8 us (6%)
  matrix products  17.5 us (6%)
  between operations  14.3 us (5%)
    ppermute x3, waiting for transfers between devices, padded_2(): lax.ppermute(tail, axis, [(i, (i + 1) % count) for i in range(ends)])  92.9 us
    all_gather x1, waiting for transfers between devices, per_device(): lax.all_gather(state_vectors, 'mem', axis=0, tiled=True)  45.6 us
    psum x1, blocking collectives, per_device(): gram_sum, pull_sum = lax.psum((gram_part, pull_part), 'rows')  42.6 us
    reshape x3, local copies, waits for them, and re-layouts, per_device(): concentration.reshape(members_dev, concentration.shape[1], rows_local * w...  19.3 us
    add x2, other arithmetic, advance(): return center + change  16 us
    reshape x2, local copies, waits for them, and re-layouts, per_device(): return updated_ensemble.reshape(concentration.shape)  14.2 us
    ppermute x3, starting transfers between devices, padded_2(): lax.ppermute(tail, axis, [(i, (i + 1) % count) for i in range(ends)])  14 us
    dot_general x1, matrix products, per_device(): jnp.einsum('jk,jzc->kzc', own_columns, lax.all_gather(state_vectors, 'mem...  13.4 us
  transfers between devices with their start and end apart: 7, of which 4 were waited for; matrix products, arithmetic and copies ran while one was open for 10% of the time, Pallas kernels for 0%

commit v1 on v0

v1 whole, which is shorter than its diff:
```python
import functools

import jax
import jax.numpy as jnp
from jax import lax
from jax.experimental import pallas as pl
from jax.experimental.pallas import tpu as pltpu
from jax.sharding import PartitionSpec as P

STEPS = 3
NS_ITERS = 4
DIFFUSION = 0.05
LANES = 128
MESH = pl.DeviceIdType.MESH
HIGHEST = lax.Precision.HIGHEST


def kernel(
    rows_n, mem_n,
    ens, cour, obs_x, obs_y, obs_value, obs_var,
    out,
    chalo, hal, coef, w0, w1, w2, w3, fc, st, prof, grec, wts, wts_s,
    c_send, c_recv, cf_send, cf_recv, h_send, h_recv,
    x_send, p_send, f_recv, q_send, q_recv, g_send, g_recv, w_sem,
):
    members, rows, levels, width = ens.shape
    total = members * mem_n
    nobs = obs_x.shape[0]
    chips = mem_n // 2
    row = lax.axis_index("rows")
    mem = lax.axis_index("mem")
    core = lax.rem(mem, 2)
    chip = mem // 2
    partner = chip * 2 + 1 - core

    def dev(r, m):
        return {"rows": r, "mem": m}

    def remote(src, dst, ssem, rsem, r, m):
        return pltpu.make_async_remote_copy(
            src_ref=src, dst_ref=dst, send_sem=ssem, recv_sem=rsem,
            device_id=(r, m), device_id_type=MESH,
        )

    barrier = pltpu.get_barrier_semaphore()
    for d in range(1, mem_n):
        pl.semaphore_signal(barrier, inc=1, device_id=(row, lax.rem(mem + d, mem_n)), device_id_type=MESH)
    for d in range(1, rows_n):
        pl.semaphore_signal(barrier, inc=1, device_id=(lax.rem(row + d, rows_n), mem), device_id_type=MESH)
    pl.semaphore_wait(barrier, mem_n - 1 + rows_n - 1)

    has_low = row > 0
    has_high = row < rows_n - 1
    low = jnp.maximum(row - 1, 0)
    high = jnp.minimum(row + 1, rows_n - 1)

    def chalo_up():
        return remote(cour.at[rows - 2 + core], chalo.at[0, core], c_send.at[0], c_recv.at[0], high, mem)

    def chalo_down():
        return remote(cour.at[core], chalo.at[1, core], c_send.at[1], c_recv.at[1], low, mem)

    def chalo_pass(side):
        return remote(chalo.at[side, core], chalo.at[side, core], cf_send.at[side], cf_recv.at[side], row, partner)

    def halo_up(m):
        return remote(ens.at[m, pl.ds(rows - 3, 3)], hal.at[m, 0], h_send.at[0, m], h_recv.at[0, m], high, mem)

    def halo_down(m):
        return remote(ens.at[m, pl.ds(0, 3)], hal.at[m, 1], h_send.at[1, m], h_recv.at[1, m], low, mem)

    @pl.when(has_high)
    def _():
        chalo_up().start()

    @pl.when(has_low)
    def _():
        chalo_down().start()

    @pl.loop(0, members)
    def _(m):
        @pl.when(has_high)
        def _():
            halo_up(m).start()

        @pl.when(has_low)
        def _():
            halo_down(m).start()

    level = lax.broadcasted_iota(jnp.int32, (levels, width), 0)
    cell = lax.broadcasted_iota(jnp.int32, (levels, width), 1)

    def set_coef(i, a0, a1, a2):
        coef[i, 0] = 1.0 - 6.0 * DIFFUSION - jnp.abs(a0) - jnp.abs(a1) - jnp.abs(a2)
        coef[i, 1] = DIFFUSION + jnp.maximum(a0, 0.0)
        coef[i, 2] = DIFFUSION - jnp.minimum(a0, 0.0)
        coef[i, 3] = jnp.where(cell > 0, DIFFUSION + jnp.maximum(a1, 0.0), 0.0)
        coef[i, 4] = jnp.where(cell < width - 1, DIFFUSION - jnp.minimum(a1, 0.0), 0.0)
        coef[i, 5] = jnp.where(level > 0, DIFFUSION + jnp.maximum(a2, 0.0), 0.0)
        coef[i, 6] = jnp.where(level < levels - 1, DIFFUSION - jnp.minimum(a2, 0.0), 0.0)

    @pl.loop(0, rows)
    def _(i):
        set_coef(i + 2, cour[i, 0], cour[i, 1], cour[i, 2])

    st[...] = jnp.zeros_like(st)

    def edge(side, present, first):
        @pl.when(present)
        def _():
            (chalo_down if side else chalo_up)().wait_recv()
            chalo_pass(side).start()
            chalo_pass(side).wait_recv()

            @pl.loop(0, 2)
            def _(i):
                set_coef(first + i, chalo[side, i, 0], chalo[side, i, 1], chalo[side, i, 2])

        @pl.when(jnp.logical_not(present))
        def _():
            coef[pl.ds(first, 2)] = jnp.zeros((2, 7, levels, width), jnp.float32)

    edge(0, has_low, 0)
    edge(1, has_high, rows + 2)

    @pl.when(jnp.logical_not(has_low))
    def _():
        w0[pl.ds(0, 3)] = jnp.zeros((3, levels, width), jnp.float32)

    @pl.when(jnp.logical_not(has_high))
    def _():
        w0[pl.ds(rows + 3, 3)] = jnp.zeros((3, levels, width), jnp.float32)

    def update(src, i, c):
        mid = src[i + 1]
        return (
            coef[c, 0] * mid
            + coef[c, 1] * src[i]
            + coef[c, 2] * src[i + 2]
            + coef[c, 3] * pltpu.roll(mid, 1, 1)
            + coef[c, 4] * pltpu.roll(mid, width - 1, 1)
            + coef[c, 5] * pltpu.roll(mid, 1, 0)
            + coef[c, 6] * pltpu.roll(mid, levels - 1, 0)
        )

    def other(d):
        return lax.rem(chip + d, chips) * 2 + core

    def send_x(d, m):
        slot = fc.at[mem * members + m]
        return remote(slot, slot, x_send.at[d, m], f_recv.at[mem, m], row, other(d))

    def send_p(d, m):
        src = lax.rem(chip + d, chips) * 2 + core
        slot = fc.at[src * members + m]
        return remote(slot, slot, p_send.at[d, m], f_recv.at[src, m], row, partner)

    def arrived(src, m):
        slot = fc.at[src * members + m]
        return remote(slot, slot, p_send.at[0, 0], f_recv.at[src, m], row, partner)

    def forward(m):
        for d in range(1, chips):
            arrived(other(d), m).wait_recv()
            send_p(d, m).start()

    lane = lax.broadcasted_iota(jnp.int32, (levels, LANES), 1)
    lag = 2

    @pl.loop(0, members)
    def _(m):
        @pl.when(has_low)
        def _():
            halo_up(m).wait_recv()
            w0[pl.ds(0, 3)] = hal[m, 0]

        @pl.when(has_high)
        def _():
            halo_down(m).wait_recv()
            w0[pl.ds(rows + 3, 3)] = hal[m, 1]

        w0[pl.ds(3, rows)] = ens[m]

        @pl.loop(0, rows + 4)
        def _(i):
            w1[i] = update(w0, i, i)

        @pl.loop(0, rows + 2)
        def _(i):
            w2[i] = update(w1, i, i + 1)

        @pl.loop(0, rows)
        def _(i):
            value = update(w2, i, i + 2)
            w3[i] = value
            fc[mem * members + m, i] = value

        @pl.loop(0, nobs)
        def _(p):
            plane = w3[obs_x[p]]
            picked = jnp.sum(jnp.where(cell == obs_y[p], plane, 0.0), axis=1, keepdims=True)
            where = pl.ds(pl.multiple_of(p * levels, levels), levels)
            st[where] = jnp.where(lane == m, picked, st[where])

        for d in range(1, chips):
            send_x(d, m).start()
        send_p(0, m).start()

        @pl.when(m >= lag)
        def _():
            forward(m - lag)

    mine = pl.ds(pl.multiple_of(mem * members, members), members)
    prof[mine] = st[...].T[:members]
    for d in range(1, mem_n):
        remote(prof.at[mine], prof.at[mine], q_send.at[d], q_recv.at[mem], row, lax.rem(mem + d, mem_n)).start()
    for d in range(1, mem_n):
        src = lax.rem(mem + d, mem_n)
        block = prof.at[pl.ds(pl.multiple_of(src * members, members), members)]
        remote(block, block, q_send.at[d], q_recv.at[src], row, src).wait_recv()

    values = prof[...]
    center = jnp.mean(values, axis=0, keepdims=True)
    scaled = (values - center) / jnp.sqrt((total - 1.0) * obs_var[...])
    innovation = (obs_value[...] - center) / jnp.sqrt(obs_var[...])
    pad = jnp.broadcast_to(innovation, (LANES - total, innovation.shape[1]))
    both = jnp.concatenate([scaled, pad], axis=0)
    grec[row] = lax.dot_general(
        scaled, both, (((1,), (1,)), ((), ())), precision=HIGHEST, preferred_element_type=jnp.float32
    )
    for d in range(1, rows_n):
        remote(grec.at[row], grec.at[row], g_send.at[d], g_recv.at[row], lax.rem(row + d, rows_n), mem).start()

    forward(members - 2)
    forward(members - 1)

    for d in range(1, rows_n):
        src = lax.rem(row + d, rows_n)
        remote(grec.at[src], grec.at[src], g_send.at[d], g_recv.at[src], src, mem).wait_recv()
    gsum = grec[0]
    for r in range(1, rows_n):
        gsum = gsum + grec[r]

    def dot(a, b):
        return jnp.dot(a, b, precision=HIGHEST, preferred_element_type=jnp.float32)

    ri = lax.broadcasted_iota(jnp.int32, (total, total), 0)
    ci = lax.broadcasted_iota(jnp.int32, (total, total), 1)
    eye = jnp.where(ri == ci, 1.0, 0.0).astype(jnp.float32)
    system = eye + gsum[:, :total]
    frob = jnp.sqrt(jnp.sum(jnp.sum(system * system, axis=1, keepdims=True), axis=0, keepdims=True))
    y = system / frob
    z = eye
    for it in range(NS_ITERS):
        factor = 0.5 * (3.0 * eye - (y if it == 0 else dot(z, y)))
        if it < NS_ITERS - 1:
            y = dot(y, factor)
        z = factor if it == 0 else dot(factor, z)
    root = z / jnp.sqrt(frob)
    shift = dot(root, dot(root, gsum))[:, total:total + 1] / jnp.sqrt(jnp.float32(total - 1.0))
    mixed = shift + root
    weights = 1.0 / total + mixed - jnp.mean(mixed, axis=0, keepdims=True)
    wts[...] = weights.T
    fetch = pltpu.make_async_copy(wts.at[mine], wts_s, w_sem)
    fetch.start()
    fetch.wait()

    for d in range(chips):
        src = lax.rem(chip + d, chips) * 2 + 1 - core

        @pl.loop(0, members)
        def _(m):
            arrived(src, m).wait_recv()

    per = 8

    @pl.loop(0, rows * (levels // per))
    def _(n):
        i = n // (levels // per)
        where = pl.ds(pl.multiple_of(lax.rem(n, levels // per) * per, per), per)

        for first in range(0, members, 16):
            count = min(16, members - first)

            def add(j, acc):
                f = fc[j, i, where]
                return tuple(acc[k] + wts_s[first + k, j] * f for k in range(count))

            acc = lax.fori_loop(
                0, total, add, tuple(jnp.zeros((per, width), jnp.float32) for _ in range(count)), unroll=2
            )
            for k in range(count):
                out[first + k, i, where] = acc[k]

    @pl.when(has_high)
    def _():
        chalo_up().wait_send()
        chalo_pass(1).wait_send()

    @pl.when(has_low)
    def _():
        chalo_down().wait_send()
        chalo_pass(0).wait_send()

    @pl.loop(0, members)
    def _(m):
        @pl.when(has_high)
        def _():
            halo_up(m).wait_send()

        @pl.when(has_low)
        def _():
            halo_down(m).wait_send()

        for d in range(1, chips):
            send_x(d, m).wait_send()
        for d in range(chips):
            send_p(d, m).wait_send()

    for d in range(1, mem_n):
        remote(prof.at[mine], prof.at[mine], q_send.at[d], q_recv.at[mem], row, lax.rem(mem + d, mem_n)).wait_send()
    for d in range(1, rows_n):
        remote(grec.at[row], grec.at[row], g_send.at[d], g_recv.at[row], lax.rem(row + d, rows_n), mem).wait_send()


def per_device(rows_n, mem_n, ensemble, courant, obs_column, obs_value, obs_var):
    members, levels, rows, width = ensemble.shape
    nobs = obs_column.shape[0]
    chips = mem_n // 2
    local = obs_column - lax.axis_index("rows") * (rows * width)
    f32 = jnp.float32
    vmem = pl.BlockSpec(memory_space=pltpu.VMEM)
    smem = pl.BlockSpec(memory_space=pltpu.SMEM)
    dma = pltpu.SemaphoreType.DMA
    total = members * mem_n
    plane = (levels, width)
    result = pl.pallas_call(
        functools.partial(kernel, rows_n, mem_n),
        out_shape=jax.ShapeDtypeStruct((members, rows, levels, width), f32),
        in_specs=[vmem, vmem, smem, smem, vmem, vmem],
        out_specs=vmem,
        scratch_shapes=[
            pltpu.VMEM((2, 2, 3) + plane, f32),
            pltpu.VMEM((members, 2, 3) + plane, f32),
            pltpu.VMEM((rows + 4, 7) + plane, f32),
            pltpu.VMEM((rows + 6,) + plane, f32),
            pltpu.VMEM((rows + 4,) + plane, f32),
            pltpu.VMEM((rows + 2,) + plane, f32),
            pltpu.VMEM((rows,) + plane, f32),
            pltpu.VMEM((total, rows) + plane, f32),
            pltpu.VMEM((nobs * levels, LANES), f32),
            pltpu.VMEM((total, nobs * levels), f32),
            pltpu.VMEM((rows_n, total, LANES), f32),
            pltpu.VMEM((total, total), f32),
            pltpu.SMEM((members, total), f32),
            dma((2,)), dma((2,)), dma((2,)), dma((2,)),
            dma((2, members)), dma((2, members)),
            dma((chips, members)), dma((chips, members)), dma((mem_n, members)),
            dma((mem_n,)), dma((mem_n,)),
            dma((rows_n,)), dma((rows_n,)),
            dma,
        ],
        compiler_params=pltpu.CompilerParams(
            collective_id=0, has_side_effects=True, vmem_limit_bytes=60 * 1024 * 1024
        ),
    )(
        ensemble.transpose(0, 2, 1, 3),
        courant.transpose(2, 0, 1, 3),
        local // width,
        local % width,
        obs_value.T.reshape(1, -1),
        obs_var.T.reshape(1, -1),
    )
    return result.transpose(0, 2, 1, 3)


def solution(mesh):
    return jax.shard_map(
        functools.partial(per_device, mesh.shape["rows"], mesh.shape["mem"]),
        mesh=mesh,
        in_specs=(
            P("mem", None, "rows", None),
            P(None, None, "rows", None),
            P("rows"),
            P(None, "rows"),
            P(None, "rows"),
        ),
        out_specs=P("mem", None, "rows", None),
        check_vma=False,
    )
```

time: 317 us -> 236 us (0.74)
  Pallas kernels: 0 us -> 225 us
  waiting for transfers between devices: 139 us -> 0 us
  blocking collectives: 53.1 us -> 0 us
  local copies, waits for them, and re-layouts: 48.7 us -> 9.86 us
  other arithmetic: 26.2 us -> 1.24 us
  starting transfers between devices: 17.8 us -> 0 us
  matrix products: 17.5 us -> 0 us
  between operations: 14.3 us -> 0.01 us
    pallas_call x0 -> x1, Pallas kernels: none -> 225 us  [per_device(): pl.pallas_call(functools.partial(kernel, rows_n, mem_n), out_shape=jax.Sh...]
    ppermute x6 -> x0, waiting for transfers between devices: 92.9 us -> none  [the longest x3 92.9 us: padded_2(): lax.ppermute(tail, axis, [(i, (i + 1) % count) for i in range(ends)])]
    all_gather x1 -> x0, waiting for transfers between devices: 45.6 us -> none  [per_device(): lax.all_gather(state_vectors, 'mem', axis=0, tiled=True)]
    psum x1 -> x0, blocking collectives: 42.6 us -> none  [per_device(): gram_sum, pull_sum = lax.psum((gram_part, pull_part), 'rows')]
    reshape x5 -> x2, local copies, waits for them, and re-layouts: 33.5 us -> 2.71 us  [the longest x1 1.36 us: per_device(): obs_var.T.reshape(1, -1)]
    ppermute x6 -> x0, starting transfers between devices: 17.8 us -> none  [the longest x3 14 us: padded_2(): lax.ppermute(tail, axis, [(i, (i + 1) % count) for i in range(ends)])]
    dot_general x18 -> x0, matrix products: 17.5 us -> none  [the longest x1 13.4 us: per_device(): jnp.einsum('jk,jzc->kzc', own_columns, lax.all_gather(state_vectors, 'mem...]
    add x2 -> x0, other arithmetic: 16 us -> none  [advance(): return center + change]
  transfers between devices with their start and end apart: 7 -> 0, of which waited for: 4 -> 0; matrix products, arithmetic and copies ran while one was open for 10% -> 0% of each run, Pallas kernels for 0% -> 0%
where the time goes in v1:
time: 236 us
  Pallas kernels  225 us (95%)
  local copies, waits for them, and re-layouts  9.86 us (4%)
    pallas_call x1, Pallas kernels, per_device(): pl.pallas_call(functools.partial(kernel, rows_n, mem_n), out_shape=jax.Sh...  225 us
    unnamed x2, local copies, waits for them, and re-layouts  7.15 us

profile of v1, /device:TPU:0, one launch (start us, length us, event | category | flops | bytes accessed | tf_op | source)
XLA Modules:
  0.0 236.0 jit_solution(3399207049528759714)
XLA Ops:
  0.0 1.2 and_select_fusion
  1.2 1.3 reshape.6.obs_value
  2.6 1.4 reshape.7.obs_var
  3.9 2.1 copy.8
  6.1 224.8 %shard_map.55 = f32[16,6,32,384]{3,2,1,0:T(8,128)} custom-call(f32[16,6,32,384]{3,2,1,0:T(8,128)} %bitcast.8, f32[6,3,32,384]{3,2,1,0:T(8,128)} %bitcast.9, s32[16]{0:T(128)} %get-tuple-element.6.obs_x, s32[16]{0:T(128)} %get-tuple-element.5.obs_y, f32[1,512]{1,0:T(1,128)} %reshape.6.obs_value, f32[1,512]{1,0:T(1,128)} %reshape.7.obs_var), custom_call_target="tpu_custom_call" | custom-call | tf_op jit(solution)/shard_map/pallas_call | solution.py:337
  230.9 5.0 %copy.10 = f32[16,32,6,384]{3,1,2,0:T(8,128)} copy(f32[16,32,6,384]{3,1,2,0:T(8,128)} %bitcast.7) | data formatting | bytes 9437184

commit v2 on v1

--- a/solution.py
+++ b/solution.py
@@ -10,6 +10,7 @@
 STEPS = 3
 NS_ITERS = 4
 DIFFUSION = 0.05
+AHEAD = 2
 LANES = 128
 MESH = pl.DeviceIdType.MESH
 HIGHEST = lax.Precision.HIGHEST
@@ -19,9 +20,9 @@
     rows_n, mem_n,
     ens, cour, obs_x, obs_y, obs_value, obs_var,
     out,
-    chalo, hal, coef, w0, w1, w2, w3, fc, st, prof, grec, wts, wts_s,
+    chalo, hal, coef, w0, w1, w2, w3, fc, st, prof, grec, wts,
     c_send, c_recv, cf_send, cf_recv, h_send, h_recv,
-    x_send, p_send, f_recv, q_send, q_recv, g_send, g_recv, w_sem,
+    x_send, p_send, f_recv, q_send, q_recv, g_send, g_recv,
 ):
     members, rows, levels, width = ens.shape
     total = members * mem_n
@@ -55,10 +56,10 @@
     high = jnp.minimum(row + 1, rows_n - 1)
 
     def chalo_up():
-        return remote(cour.at[rows - 2 + core], chalo.at[0, core], c_send.at[0], c_recv.at[0], high, mem)
+        return remote(cour.at[:, rows - 2 + core], chalo.at[0, core], c_send.at[0], c_recv.at[0], high, mem)
 
     def chalo_down():
-        return remote(cour.at[core], chalo.at[1, core], c_send.at[1], c_recv.at[1], low, mem)
+        return remote(cour.at[:, core], chalo.at[1, core], c_send.at[1], c_recv.at[1], low, mem)
 
     def chalo_pass(side):
         return remote(chalo.at[side, core], chalo.at[side, core], cf_send.at[side], cf_recv.at[side], row, partner)
@@ -77,15 +78,20 @@
     def _():
         chalo_down().start()
 
-    @pl.loop(0, members)
+    def send_halo(m):
+        @pl.when(has_high)
+        def _():
+            halo_up(m).start()
+
+        @pl.when(has_low)
+        def _():
+            halo_down(m).start()
+
+    ahead = min(AHEAD, members)
+
+    @pl.loop(0, ahead)
     def _(m):
-        @pl.when(has_high)
-        def _():
-            halo_up(m).start()
-
-        @pl.when(has_low)
-        def _():
-            halo_down(m).start()
+        send_halo(m)
 
     level = lax.broadcasted_iota(jnp.int32, (levels, width), 0)
     cell = lax.broadcasted_iota(jnp.int32, (levels, width), 1)
@@ -101,7 +107,7 @@
 
     @pl.loop(0, rows)
     def _(i):
-        set_coef(i + 2, cour[i, 0], cour[i, 1], cour[i, 2])
+        set_coef(i + 2, cour[0, i], cour[1, i], cour[2, i])
 
     st[...] = jnp.zeros_like(st)
 
@@ -179,6 +185,10 @@
             halo_down(m).wait_recv()
             w0[pl.ds(rows + 3, 3)] = hal[m, 1]
 
+        @pl.when(m + ahead < members)
+        def _():
+            send_halo(m + ahead)
+
         w0[pl.ds(3, rows)] = ens[m]
 
         @pl.loop(0, rows + 4)
@@ -198,7 +208,8 @@
         @pl.loop(0, nobs)
         def _(p):
             plane = w3[obs_x[p]]
-            picked = jnp.sum(jnp.where(cell == obs_y[p], plane, 0.0), axis=1, keepdims=True)
+            hit = cell == obs_y[p]
+            picked = jnp.sum(jnp.where(hit, plane, 0.0), axis=1, keepdims=True)
             where = pl.ds(pl.multiple_of(p * levels, levels), levels)
             st[where] = jnp.where(lane == m, picked, st[where])
 
@@ -209,6 +220,18 @@
         @pl.when(m >= lag)
         def _():
             forward(m - lag)
+
+    def dot(a, b):
+        return jnp.dot(a, b, precision=HIGHEST, preferred_element_type=jnp.float32)
+
+    def flat(ref):
+        n = nobs * levels
+        spread = lax.broadcasted_iota(jnp.int32, (levels, n), 1) % levels
+        spread = jnp.where(spread == lax.broadcasted_iota(jnp.int32, (levels, n), 0), 1.0, 0.0)
+        wide = dot(ref[...], spread.astype(jnp.float32))
+        owner = lax.broadcasted_iota(jnp.int32, (nobs, n), 1) // levels
+        own = owner == lax.broadcasted_iota(jnp.int32, (nobs, n), 0)
+        return jnp.sum(jnp.where(own, wide, 0.0), axis=0, keepdims=True)
 
     mine = pl.ds(pl.multiple_of(mem * members, members), members)
     prof[mine] = st[...].T[:members]
@@ -220,9 +243,10 @@
         remote(block, block, q_send.at[d], q_recv.at[src], row, src).wait_recv()
 
     values = prof[...]
+    variance = flat(obs_var)
     center = jnp.mean(values, axis=0, keepdims=True)
-    scaled = (values - center) / jnp.sqrt((total - 1.0) * obs_var[...])
-    innovation = (obs_value[...] - center) / jnp.sqrt(obs_var[...])
+    scaled = (values - center) / jnp.sqrt((total - 1.0) * variance)
+    innovation = (flat(obs_value) - center) / jnp.sqrt(variance)
     pad = jnp.broadcast_to(innovation, (LANES - total, innovation.shape[1]))
     both = jnp.concatenate([scaled, pad], axis=0)
     grec[row] = lax.dot_general(
@@ -240,9 +264,6 @@
     gsum = grec[0]
     for r in range(1, rows_n):
         gsum = gsum + grec[r]
-
-    def dot(a, b):
-        return jnp.dot(a, b, precision=HIGHEST, preferred_element_type=jnp.float32)
 
     ri = lax.broadcasted_iota(jnp.int32, (total, total), 0)
     ci = lax.broadcasted_iota(jnp.int32, (total, total), 1)
@@ -261,9 +282,21 @@
     mixed = shift + root
     weights = 1.0 / total + mixed - jnp.mean(mixed, axis=0, keepdims=True)
     wts[...] = weights.T
-    fetch = pltpu.make_async_copy(wts.at[mine], wts_s, w_sem)
-    fetch.start()
-    fetch.wait()
+    tile = 8
+    outs, ins = members * tile, total * tile
+
+    def hot(shape, dim, size):
+        big = lax.broadcasted_iota(jnp.int32, shape, dim) // size
+        return jnp.where(big == lax.broadcasted_iota(jnp.int32, shape, 1 - dim), 1.0, 0.0).astype(jnp.float32)
+
+    wide = dot(dot(hot((outs, members), 0, tile), wts[mine]), hot((total, ins), 1, tile))
+    same = (
+        lax.broadcasted_iota(jnp.int32, (outs, ins), 0) % tile
+        == lax.broadcasted_iota(jnp.int32, (outs, ins), 1) % tile
+    )
+    wide = jnp.where(same, wide, 0.0)
+    wide_high = wide.astype(jnp.bfloat16)
+    wide_low = (wide - wide_high.astype(jnp.float32)).astype(jnp.bfloat16)
 
     for d in range(chips):
         src = lax.rem(chip + d, chips) * 2 + 1 - core
@@ -272,25 +305,18 @@
         def _(m):
             arrived(src, m).wait_recv()
 
-    per = 8
-
-    @pl.loop(0, rows * (levels // per))
+    def dot16(a, b):
+        return jnp.dot(a, b, preferred_element_type=jnp.float32)
+
+    @pl.loop(0, rows * (levels // tile))
     def _(n):
-        i = n // (levels // per)
-        where = pl.ds(pl.multiple_of(lax.rem(n, levels // per) * per, per), per)
-
-        for first in range(0, members, 16):
-            count = min(16, members - first)
-
-            def add(j, acc):
-                f = fc[j, i, where]
-                return tuple(acc[k] + wts_s[first + k, j] * f for k in range(count))
-
-            acc = lax.fori_loop(
-                0, total, add, tuple(jnp.zeros((per, width), jnp.float32) for _ in range(count)), unroll=2
-            )
-            for k in range(count):
-                out[first + k, i, where] = acc[k]
+        i = n // (levels // tile)
+        where = pl.ds(pl.multiple_of(lax.rem(n, levels // tile) * tile, tile), tile)
+        f = fc[:, i, where].reshape(ins, width)
+        f_high = f.astype(jnp.bfloat16)
+        f_low = (f - f_high.astype(jnp.float32)).astype(jnp.bfloat16)
+        value = dot16(wide_high, f_high) + (dot16(wide_high, f_low) + dot16(wide_low, f_high))
+        out[:, i, where] = value.reshape(members, tile, width)
 
     @pl.when(has_high)
     def _():
@@ -352,24 +378,22 @@
             pltpu.VMEM((total, nobs * levels), f32),
             pltpu.VMEM((rows_n, total, LANES), f32),
             pltpu.VMEM((total, total), f32),
-            pltpu.SMEM((members, total), f32),
             dma((2,)), dma((2,)), dma((2,)), dma((2,)),
             dma((2, members)), dma((2, members)),
             dma((chips, members)), dma((chips, members)), dma((mem_n, members)),
             dma((mem_n,)), dma((mem_n,)),
             dma((rows_n,)), dma((rows_n,)),
-            dma,
         ],
         compiler_params=pltpu.CompilerParams(
             collective_id=0, has_side_effects=True, vmem_limit_bytes=60 * 1024 * 1024
         ),
     )(
         ensemble.transpose(0, 2, 1, 3),
-        courant.transpose(2, 0, 1, 3),
+        courant.transpose(0, 2, 1, 3),
         local // width,
         local % width,
-        obs_value.T.reshape(1, -1),
-        obs_var.T.reshape(1, -1),
+        obs_value.T,
+        obs_var.T,
     )
     return result.transpose(0, 2, 1, 3)
 

time: 236 us -> 170 us (0.72)
  Pallas kernels: 225 us -> 163 us
  local copies, waits for them, and re-layouts: 9.86 us -> 5.01 us
    pallas_call x1, Pallas kernels: 225 us -> 163 us  [per_device(): pl.pallas_call(functools.partial(kernel, rows_n, mem_n), out_shape=jax.Sh...]
    reshape x2 -> x0, local copies, waits for them, and re-layouts: 2.71 us -> none  [the longest x1 1.36 us: per_device(): obs_var.T.reshape(1, -1)]
    unnamed x2 -> x1, local copies, waits for them, and re-layouts: 7.15 us -> 5.01 us
where the time goes in v2:
time: 170 us
  Pallas kernels  163 us (96%)
  local copies, waits for them, and re-layouts  5.01 us (3%)
    pallas_call x1, Pallas kernels, per_device(): pl.pallas_call(functools.partial(kernel, rows_n, mem_n), out_shape=jax.Sh...  163 us
    unnamed x1, local copies, waits for them, and re-layouts  5.01 us

profile of v2, /device:TPU:0, one launch (start us, length us, event | category | flops | bytes accessed | tf_op | source)
XLA Modules:
  0.0 169.6 jit_solution(16489129474246231238)
XLA Ops:
  0.0 1.2 and_select_fusion
  1.2 163.3 %shard_map.55 = f32[16,6,32,384]{3,2,1,0:T(8,128)} custom-call(f32[16,6,32,384]{3,2,1,0:T(8,128)} %bitcast.6, f32[3,6,32,384]{3,2,1,0:T(8,128)} %bitcast.7, s32[16]{0:T(128)} %get-tuple-element.6.obs_x, s32[16]{0:T(128)} %get-tuple-element.5.obs_y, f32[16,32]{1,0:T(8,128)} %bitcast.8, f32[16,32]{1,0:T(8,128)} %bitcast.9), custom_call_target="tpu_custom_call" | custom-call | tf_op jit(solution)/shard_map/pallas_call | solution.py:363
  164.6 5.0 %copy.7 = f32[16,32,6,384]{3,1,2,0:T(8,128)} copy(f32[16,32,6,384]{3,1,2,0:T(8,128)} %bitcast.5) | data formatting | bytes 9437184

commit v3 on v2

--- a/solution.py
+++ b/solution.py
@@ -191,21 +191,21 @@
 
         w0[pl.ds(3, rows)] = ens[m]
 
-        @pl.loop(0, rows + 4)
+        @pl.loop(0, rows + 4, unroll=2)
         def _(i):
             w1[i] = update(w0, i, i)
 
-        @pl.loop(0, rows + 2)
+        @pl.loop(0, rows + 2, unroll=2)
         def _(i):
             w2[i] = update(w1, i, i + 1)
 
-        @pl.loop(0, rows)
+        @pl.loop(0, rows, unroll=2)
         def _(i):
             value = update(w2, i, i + 2)
             w3[i] = value
             fc[mem * members + m, i] = value
 
-        @pl.loop(0, nobs)
+        @pl.loop(0, nobs, unroll=4)
         def _(p):
             plane = w3[obs_x[p]]
             hit = cell == obs_y[p]
@@ -308,7 +308,7 @@
     def dot16(a, b):
         return jnp.dot(a, b, preferred_element_type=jnp.float32)
 
-    @pl.loop(0, rows * (levels // tile))
+    @pl.loop(0, rows * (levels // tile), unroll=2)
     def _(n):
         i = n // (levels // tile)
         where = pl.ds(pl.multiple_of(lax.rem(n, levels // tile) * tile, tile), tile)

time: 170 us -> 166 us (0.976)
  Pallas kernels: 163 us -> 159 us
    pallas_call x1, Pallas kernels: 163 us -> 159 us  [per_device(): pl.pallas_call(functools.partial(kernel, rows_n, mem_n), out_shape=jax.Sh...]
where the time goes in v3:
time: 166 us
  Pallas kernels  159 us (96%)
  local copies, waits for them, and re-layouts  5.01 us (3%)
    pallas_call x1, Pallas kernels, per_device(): pl.pallas_call(functools.partial(kernel, rows_n, mem_n), out_shape=jax.Sh...  159 us
    unnamed x1, local copies, waits for them, and re-layouts  5.01 us

profile of v3, /device:TPU:0, one launch (start us, length us, event | category | flops | bytes accessed | tf_op | source)
XLA Modules:
  0.0 165.7 jit_solution(7812569074525189902)
XLA Ops:
  0.0 1.2 and_select_fusion
  1.2 159.5 %shard_map.55 = f32[16,6,32,384]{3,2,1,0:T(8,128)} custom-call(f32[16,6,32,384]{3,2,1,0:T(8,128)} %bitcast.6, f32[3,6,32,384]{3,2,1,0:T(8,128)} %bitcast.7, s32[16]{0:T(128)} %get-tuple-element.6.obs_x, s32[16]{0:T(128)} %get-tuple-element.5.obs_y, f32[16,32]{1,0:T(8,128)} %bitcast.8, f32[16,32]{1,0:T(8,128)} %bitcast.9), custom_call_target="tpu_custom_call" | custom-call | tf_op jit(solution)/shard_map/pallas_call | solution.py:363
  160.7 5.0 %copy.7 = f32[16,32,6,384]{3,1,2,0:T(8,128)} copy(f32[16,32,6,384]{3,1,2,0:T(8,128)} %bitcast.5) | data formatting | bytes 9437184
